TPU v7x, 32 devices: a whole 2x2x4 slice. The times are simulated.
32 devices in a mesh: dp: 16 (over z, y, x), feat: 2 (over core).
Axes of the slice: x: 2, y: 2, z: 4, core: 2. Of those that a mesh axis runs over, the one named last changes fastest.
Arguments:
- samples: bfloat16 [4096, 16384], P('dp', 'feat'), may hold values from -1 to 1
- labels: int32 [4096], P('dp'), may hold values from -1 to 1, as said below
- dual: float32 [4096], P('dp'), may hold values from 0 to 1
- counts: int32 [16], P('dp'), may hold values from 1 to 2, as said below
- order: int32 [16, 2], P('dp'), may hold values from 0 to 1, each once within a row
- weights: float32 [16384], P('feat'), may hold values from -0.046875 to 0.046875
Outputs:
- weights_new: float32 [16384], P('feat')
- dual_new: float32 [4096], P('dp')
- margins: float32 [4096], P('dp')
- gap: float32 [], replicated
Inputs may be any that keep to these rules, and one draw needn't show every extreme that they name: `labels`: each entry is -1 or 1. `counts`: some index of dp has exactly 2 live blocks.
All inputs are finite; a program needn't handle non-finite values.
Results may differ from a plain program's by a relative error of at most 0.003.
Values sent between devices are 32-bit elements; how exact they have to be, the bound alone decides.
A program may use at most 64 MiB of HBM per device.

v0:
```python
import jax
import jax.numpy as jnp
from jax import lax
from jax.sharding import PartitionSpec as P

BLOCK = 128
CAP = 2
PASSES = 2


def block_solve(system, right):
    factor = jnp.linalg.cholesky(system)
    lower_part = lax.linalg.triangular_solve(factor, right[:, None], left_side=True, lower=True)
    result = lax.linalg.triangular_solve(
        factor, lower_part, left_side=True, lower=True, transpose_a=True
    )
    return result[:, 0]


def body(samples, labels, dual, counts, order, weights):
    reg = 1.0 / 384.0
    groups = lax.axis_size("dp")
    half = samples.shape[1]
    blocks_x = samples.reshape(CAP, BLOCK, half)
    total = lax.psum(counts[0].astype(jnp.float32), "dp") * BLOCK
    scale = groups / (reg * total)
    count = counts[0]
    partial_grams = jnp.einsum(
        "brd,bsd->brs", blocks_x, blocks_x, preferred_element_type=jnp.float32
    )
    grams = lax.psum(partial_grams, "feat")

    def advance(step, carry):
        beta, change = carry
        slot = order[0, step % CAP]
        rows = lax.dynamic_index_in_dim(blocks_x, slot, 0, keepdims=False)
        vector = (weights + change).astype(jnp.bfloat16)
        partial_margin = jnp.dot(rows, vector, preferred_element_type=jnp.float32)
        margin = lax.psum(partial_margin, "feat")
        gram = lax.dynamic_index_in_dim(grams, slot, 0, keepdims=False)
        start = slot * BLOCK
        signs = lax.dynamic_slice_in_dim(labels, start, BLOCK).astype(jnp.float32)
        before = lax.dynamic_slice_in_dim(beta, start, BLOCK)
        system = (
            jnp.eye(BLOCK, dtype=jnp.float32) + scale * (signs[:, None] * signs[None, :]) * gram
        )
        delta = block_solve(system, 1.0 - before - signs * margin)
        after = jnp.where(slot < count, jnp.maximum(before + delta, 0.0), before)
        scaled = (signs * (after - before)).astype(jnp.bfloat16)
        change = change + scale * jnp.dot(scaled, rows, preferred_element_type=jnp.float32)
        beta = lax.dynamic_update_slice_in_dim(beta, after, start, 0)
        return (beta, change)

    beta, change = lax.fori_loop(0, PASSES * CAP, advance, (dual, jnp.zeros((half,), jnp.float32)))
    summed = lax.psum(change, "dp")
    weights_new = weights + summed / groups
    first_group = (lax.axis_index("dp") == 0).astype(jnp.float32)
    norm_part = jnp.sum(weights_new * weights_new) * first_group
    partial_scores = jnp.dot(
        samples, weights_new.astype(jnp.bfloat16), preferred_element_type=jnp.float32
    )
    margins = lax.psum(partial_scores, "feat")
    slots = jnp.arange(CAP * BLOCK, dtype=jnp.int32)
    live = slots // BLOCK < count
    signs = labels.astype(jnp.float32)
    hinge = jnp.maximum(1.0 - signs * margins, 0.0)
    first_half = (lax.axis_index("feat") == 0).astype(jnp.float32)
    loss_part = jnp.sum(jnp.where(live, 0.5 * hinge * hinge, 0.0)) * first_half
    dual_part = jnp.sum(jnp.where(live, beta - 0.5 * beta * beta, 0.0)) * first_half
    loss, dualsum, norm = lax.psum((loss_part, dual_part, norm_part), ("dp", "feat"))
    gap = reg * norm + (loss - dualsum) / total
    return (weights_new, beta, margins, gap)


def solution(mesh):
    return jax.shard_map(
        body,
        mesh=mesh,
        in_specs=(P("dp", "feat"), P("dp"), P("dp"), P("dp"), P("dp", None), P("feat")),
        out_specs=(P("feat"), P("dp"), P("dp"), P()),
        check_vma=False,
    )
```

profile of v0, /device:TPU:12, one launch (start us, length us, event | category | flops | bytes accessed | tf_op | source)
XLA Modules:
  0.0 335.4 jit_solution(18046364474905601856)
XLA Ops:
  7.3 5.4 %fusion.36 = f32[2,128,128]{2,1,0:T(8,128)} fusion(bf16[2,128,8192]{2,1,0:T(8,128)(2,1)} %bitcast.91), kind=kOutput, calls=%fused_computation.55 | convolution fusion | flops 536870912 | bytes 4325376 | tf_op jit(solution)/shard_map/brd,bsd->brs/dot_general | solution.py:28
  13.3 32.5 %psum.63 = f32[]{:T(128)} all-reduce(f32[]{:T(128)S(6)} %convert_element_type.51), channel_id=1, replica_groups=mesh['dp'=16,'feat'=2] {'dp'}, use_global_device_ids=true, to_apply=%region_1.0 | all-reduce | flops 1 | bytes 8 | tf_op jit(solution)/shard_map/psum | solution.py:25
  46.6 147.6 %while.18 = (s32[]{:T(128)}, f32[256]{0:T(256)S(1)}, f32[8192]{0:T(1024)S(1)}, s32[1,2]{1,0:T(1,128)S(1)}, s32[]{:T(128)}, /*index=5*/f32[]{:T(128)}, s32[256]{0...) while((s32[]{:T(128)}, f32[256]{0:T(256)S(1)}, ...), condition=%wide.region_6.7_spmd.clone, body=%wide.region_2.6_spmd.clone.sunk | while | flops 4982547 | bytes 5255052 | solution.py:54
  46.6 0.6 constant_dynamic-slice_fusion.2
  49.9 0.9 fusion.66
  50.9 0.9 fusion.67
  51.8 11.7 %cholesky.78 = f32[128,128]{1,0:T(8,128)S(1)} custom-call(f32[128,128]{1,0:T(8,128)S(1)} %fusion.67), custom_call_target="Cholesky" | custom-call | tf_op jit(solution)/shard_map/while/body/eval_jaxpr/jit(cholesky)/cholesky | solution.py:12
  63.6 0.6 compare_reduce_fusion.2
  64.2 0.7 fusion.68
  64.9 9.8 %custom-call.25 = f32[1,128,128]{1,2,0:T(8,128)S(1)} custom-call(f32[1,128,128]{2,1,0:T(8,128)S(1)} %fusion.68), custom_call_target="InvertDiagBlocksLowerTriangular" | custom-call | tf_op jit(solution)/shard_map/while/body/eval_jaxpr/triangular_solve | solution.py:14
  74.8 2.2 fusion.69
  77.0 2.5 psum.72
  79.4 0.2 convolution_bitcast_fusion.3
  81.0 0.2 fusion.70
  81.2 2.1 fusion.71
  83.3 0.2 dynamic_update_slice.12
  83.5 0.6 constant_dynamic-slice_fusion.2
  86.8 0.9 fusion.66
  87.8 0.9 fusion.67
  88.7 11.7 %cholesky.78 = f32[128,128]{1,0:T(8,128)S(1)} custom-call(f32[128,128]{1,0:T(8,128)S(1)} %fusion.67), custom_call_target="Cholesky" | custom-call | tf_op jit(solution)/shard_map/while/body/eval_jaxpr/jit(cholesky)/cholesky | solution.py:12
  100.5 0.6 compare_reduce_fusion.2
  101.1 0.7 fusion.68
  101.8 9.8 %custom-call.25 = f32[1,128,128]{1,2,0:T(8,128)S(1)} custom-call(f32[1,128,128]{2,1,0:T(8,128)S(1)} %fusion.68), custom_call_target="InvertDiagBlocksLowerTriangular" | custom-call | tf_op jit(solution)/shard_map/while/body/eval_jaxpr/triangular_solve | solution.py:14
  111.6 2.2 fusion.69
  113.9 2.5 psum.72
  116.3 0.2 convolution_bitcast_fusion.3
  117.9 0.2 fusion.70
  118.1 2.1 fusion.71
  120.2 0.2 dynamic_update_slice.12
  120.4 0.6 constant_dynamic-slice_fusion.2
  123.7 0.9 fusion.66
  124.6 0.1 copy.12
  124.7 0.9 fusion.67
  125.6 11.7 %cholesky.78 = f32[128,128]{1,0:T(8,128)S(1)} custom-call(f32[128,128]{1,0:T(8,128)S(1)} %fusion.67), custom_call_target="Cholesky" | custom-call | tf_op jit(solution)/shard_map/while/body/eval_jaxpr/jit(cholesky)/cholesky | solution.py:12
  137.4 0.6 compare_reduce_fusion.2
  138.0 0.7 fusion.68
  138.7 9.8 %custom-call.25 = f32[1,128,128]{1,2,0:T(8,128)S(1)} custom-call(f32[1,128,128]{2,1,0:T(8,128)S(1)} %fusion.68), custom_call_target="InvertDiagBlocksLowerTriangular" | custom-call | tf_op jit(solution)/shard_map/while/body/eval_jaxpr/triangular_solve | solution.py:14
  148.5 2.2 fusion.69
  150.8 2.5 psum.72
  153.2 0.2 convolution_bitcast_fusion.3
  154.8 0.2 fusion.70
  155.0 2.1 fusion.71
  157.0 0.2 dynamic_update_slice.12
  157.3 0.6 constant_dynamic-slice_fusion.2
  160.6 0.9 fusion.66
  161.5 0.1 copy.12
  161.6 0.9 fusion.67
  162.5 11.7 %cholesky.78 = f32[128,128]{1,0:T(8,128)S(1)} custom-call(f32[128,128]{1,0:T(8,128)S(1)} %fusion.67), custom_call_target="Cholesky" | custom-call | tf_op jit(solution)/shard_map/while/body/eval_jaxpr/jit(cholesky)/cholesky | solution.py:12
  174.3 0.6 compare_reduce_fusion.2
  174.9 0.7 fusion.68
  175.6 9.8 %custom-call.25 = f32[1,128,128]{1,2,0:T(8,128)S(1)} custom-call(f32[1,128,128]{2,1,0:T(8,128)S(1)} %fusion.68), custom_call_target="InvertDiagBlocksLowerTriangular" | custom-call | tf_op jit(solution)/shard_map/while/body/eval_jaxpr/triangular_solve | solution.py:14
  185.4 2.2 fusion.69
  187.7 2.5 psum.72
  190.1 0.2 convolution_bitcast_fusion.3
  191.7 0.2 fusion.70
  191.9 2.1 fusion.71
  193.9 0.2 dynamic_update_slice.12
  194.2 71.7 %psum.65 = f32[8192]{0:T(1024)S(1)} all-reduce(f32[8192]{0:T(1024)S(1)} %get-tuple-element.248), channel_id=1, replica_groups=mesh['dp'=16,'feat'=2] {'dp'}, use_global_device_ids=true, to_apply=%region_7.8 | all-reduce | flops 8192 | bytes 65536 | tf_op jit(solution)/shard_map/psum | solution.py:55
  265.9 0.6 multiply_reduce_fusion
  266.6 3.4 %fusion.37 = f32[1,256]{1,0:T(1,128)S(1)} fusion(bf16[8192,1]{0,1:T(2,128)(2,1)S(1)} %reshape.63, bf16[256,8192]{1,0:T(8,128)(2,1)} %bitcast.93), kind=kOutput, calls=%fused_computation.56 | convolution fusion | flops 4194304 | bytes 4211712 | tf_op jit(solution)/shard_map/dot_general | solution.py:59
  269.9 2.5 psum.66
  272.4 0.7 fusion.32
  273.1 0.6 fusion.35
  276.2 49.2 %all-reduce = (f32[]{:T(128)}, f32[]{:T(128)}, f32[]{:T(128)}) all-reduce(f32[]{:T(128)S(6)} %mul.160, f32[]{:T(128)S(6)} %mul.165, f32[]{:T(128)S(6)} %mul.168), channel_id=1, replica_groups=mesh['dp'=16,'feat'=2] {'dp','feat'}, use_global_device_ids=true, to_apply=%region_10.11 | all-reduce | flops 3 | bytes 24 | tf_op jit(solution)/shard_map/psum | solution.py:70
  (42 shorter events, 0.9 us)
Async XLA Ops:
  7.2 39.4 %all-reduce.3.cloned.1.call-start = ((), (), s32[]{:S(2)}) async-start(), calls=%async_computation | async-start | bytes 262144 | tf_op jit(solution)/shard_map/psum | solution.py:31
  7.2 39.3 %copy-start = (f32[8192]{0:T(1024)S(1)}, f32[8192]{0:T(1024)}, u32[]{:S(2)}) copy-start(f32[8192]{0:T(1024)} %param.13) | copy-start | bytes 98308
  7.2 39.3 %copy-start.3 = (f32[256]{0:T(256)S(1)}, f32[256]{0:T(256)}, u32[]{:S(2)}) copy-start(f32[256]{0:T(256)} %param.10) | copy-start | bytes 3076
  7.2 39.3 %copy-start.4 = (s32[256]{0:T(256)S(1)}, s32[256]{0:T(256)}, u32[]{:S(2)}) copy-start(s32[256]{0:T(256)} %param.9) | copy-start | bytes 3076
  7.2 39.3 %copy-start.6 = (s32[1,2]{1,0:T(1,128)S(1)}, s32[1,2]{1,0:T(1,128)}, u32[]{:S(2)}) copy-start(s32[1,2]{1,0:T(1,128)} %param.12) | copy-start | bytes 28
  194.2 133.2 %copy-start.2 = (f32[256]{0:T(256)}, f32[256]{0:T(256)S(1)}, u32[]{:S(2)}) copy-start(f32[256]{0:T(256)S(1)} %get-tuple-element.245) | copy-start | bytes 3076
  266.5 60.8 %copy-start.1 = (f32[8192]{0:T(1024)}, f32[8192]{0:T(1024)S(1)}, u32[]{:S(2)}) copy-start(f32[8192]{0:T(1024)S(1)} %get-tuple-element.307) | copy-start | bytes 98308
  272.4 55.0 %copy-start.5 = (f32[256]{0:T(256)}, f32[256]{0:T(256)S(1)}, u32[]{:S(2)}) copy-start(f32[256]{0:T(256)S(1)} %psum.66) | copy-start | bytes 3076
Sparse Core Ops, SparseCore 0:
  12.8 19.3 all-reduce.2
where the time goes:
time: 337 us; the launch traced here: 335 us
  blocking collectives  166 us (49%)
  other arithmetic  101 us (30%)
  matrix products  27.6 us (8%)
  between operations  21 us (6%)
  loops' own time  16 us (5%)
  local copies, waits for them, and re-layouts  3.78 us (1%)
    psum x1, blocking collectives, body(): summed = lax.psum(change, 'dp')  71.7 us
    another operation x12, other arithmetic, block_solve(): factor = jnp.linalg.cholesky(system)  49.6 us
    psum x1, blocking collectives, body(): lax.psum((loss_part, dual_part, norm_part), ('dp', 'feat'))  49.2 us
    another operation x8, other arithmetic, block_solve(): lax.linalg.triangular_solve(factor, lower_part, left_side=True, lower=Tru...  41.9 us
    psum x1, blocking collectives, body(): total = lax.psum(counts[0].astype(jnp.float32), 'dp') * BLOCK  32.5 us
    another operation x1, loops' own time, body(): lax.fori_loop(0, PASSES * CAP, advance, (dual, jnp.zeros((half,), jnp.flo...  16 us
    psum x4, blocking collectives, advance(): margin = lax.psum(partial_margin, 'feat')  9.85 us
    dot_general x4, matrix products, advance(): partial_margin = jnp.dot(rows, vector, preferred_element_type=jnp.float32)  8.94 us
  transfers between devices with their start and end apart: 1, of which 0 were waited for; matrix products, arithmetic and copies ran while one was open for 0% of the time, Pallas kernels for 0%

commit v1 on v0

--- a/solution.py
+++ b/solution.py
@@ -22,7 +22,7 @@
     groups = lax.axis_size("dp")
     half = samples.shape[1]
     blocks_x = samples.reshape(CAP, BLOCK, half)
-    total = lax.psum(counts[0].astype(jnp.float32), "dp") * BLOCK
+    total = jnp.sum(lax.all_gather(counts[0].astype(jnp.float32), "dp"), axis=0) * BLOCK
     scale = groups / (reg * total)
     count = counts[0]
     partial_grams = jnp.einsum(

time: 337 us -> 338 us (level)
    psum x1 -> x0, blocking collectives: 32.5 us -> none  [body(): total = lax.psum(counts[0].astype(jnp.float32), 'dp') * BLOCK]
    unnamed x0 -> x1, blocking collectives: none -> 32 us
  transfers between devices with their start and end apart: 1 -> 1, of which waited for: 0 -> 0; matrix products, arithmetic and copies ran while one was open for 0% -> 1% of each run, Pallas kernels for 0% -> 0%
where the time goes in v1:
time: 338 us; the launch traced here: 337 us
  blocking collectives  165 us (49%)
  other arithmetic  102 us (30%)
  matrix products  27.6 us (8%)
  between operations  21.2 us (6%)
  loops' own time  16 us (5%)
  local copies, waits for them, and re-layouts  5.13 us (2%)
    psum x1, blocking collectives, body(): summed = lax.psum(change, 'dp')  71.7 us
    another operation x12, other arithmetic, block_solve(): factor = jnp.linalg.cholesky(system)  49.6 us
    psum x1, blocking collectives, body(): lax.psum((loss_part, dual_part, norm_part), ('dp', 'feat'))  49.2 us
    another operation x8, other arithmetic, block_solve(): lax.linalg.triangular_solve(factor, lower_part, left_side=True, lower=Tru...  41.9 us
    unnamed x1, blocking collectives  32 us
    another operation x1, loops' own time, body(): lax.fori_loop(0, PASSES * CAP, advance, (dual, jnp.zeros((half,), jnp.flo...  16 us
    psum x4, blocking collectives, advance(): margin = lax.psum(partial_margin, 'feat')  9.85 us
    dot_general x4, matrix products, advance(): partial_margin = jnp.dot(rows, vector, preferred_element_type=jnp.float32)  8.94 us
  transfers between devices with their start and end apart: 1, of which 0 were waited for; matrix products, arithmetic and copies ran while one was open for 1% of the time, Pallas kernels for 0%

profile of v1, /device:TPU:12, one launch (start us, length us, event | category | flops | bytes accessed | tf_op | source)
XLA Modules:
  0.0 337.1 jit_solution(3971166078038194759)
XLA Ops:
  7.3 5.4 %fusion.36 = f32[2,128,128]{2,1,0:T(8,128)} fusion(bf16[2,128,8192]{2,1,0:T(8,128)(2,1)} %bitcast.93), kind=kOutput, calls=%fused_computation.55 | convolution fusion | flops 536870912 | bytes 4325376 | tf_op jit(solution)/shard_map/brd,bsd->brs/dot_general | solution.py:28
  13.4 0.6 dynamic-slice
  13.9 0.8 dynamic-update-slice.5
  14.7 32.0 %all-reduce = f32[16]{0:T(128)S(1)} all-reduce(f32[16]{0:T(128)S(1)} %dynamic-update-slice.5), channel_id=1, replica_groups=mesh['dp'=16,'feat'=2] {'dp'}, use_global_device_ids=true, to_apply=%add | all-reduce | flops 16 | bytes 128
  46.7 0.7 reduce_sum.36
  48.1 147.6 %while.18 = (s32[]{:T(128)}, f32[256]{0:T(256)S(1)}, f32[8192]{0:T(1024)S(1)}, s32[1,2]{1,0:T(1,128)S(1)}, s32[]{:T(128)}, /*index=5*/f32[]{:T(128)}, s32[256]{0...) while((s32[]{:T(128)}, f32[256]{0:T(256)S(1)}, ...), condition=%wide.region_6.7_spmd.clone, body=%wide.region_2.6_spmd.clone.sunk | while | flops 4982547 | bytes 5255052 | solution.py:54
  48.1 0.6 constant_dynamic-slice_fusion.2
  51.3 0.9 fusion.66
  52.4 0.9 fusion.67
  53.3 11.7 %cholesky.78 = f32[128,128]{1,0:T(8,128)S(1)} custom-call(f32[128,128]{1,0:T(8,128)S(1)} %fusion.67), custom_call_target="Cholesky" | custom-call | tf_op jit(solution)/shard_map/while/body/eval_jaxpr/jit(cholesky)/cholesky | solution.py:12
  65.0 0.6 compare_reduce_fusion.2
  65.7 0.7 fusion.68
  66.4 9.8 %custom-call.25 = f32[1,128,128]{1,2,0:T(8,128)S(1)} custom-call(f32[1,128,128]{2,1,0:T(8,128)S(1)} %fusion.68), custom_call_target="InvertDiagBlocksLowerTriangular" | custom-call | tf_op jit(solution)/shard_map/while/body/eval_jaxpr/triangular_solve | solution.py:14
  76.2 2.2 fusion.69
  78.5 2.5 psum.64
  80.9 0.2 convolution_bitcast_fusion.3
  82.4 0.2 fusion.70
  82.6 2.1 fusion.71
  84.7 0.2 dynamic_update_slice.12
  85.0 0.6 constant_dynamic-slice_fusion.2
  88.2 0.9 fusion.66
  89.3 0.9 fusion.67
  90.2 11.7 %cholesky.78 = f32[128,128]{1,0:T(8,128)S(1)} custom-call(f32[128,128]{1,0:T(8,128)S(1)} %fusion.67), custom_call_target="Cholesky" | custom-call | tf_op jit(solution)/shard_map/while/body/eval_jaxpr/jit(cholesky)/cholesky | solution.py:12
  101.9 0.6 compare_reduce_fusion.2
  102.6 0.7 fusion.68
  103.2 9.8 %custom-call.25 = f32[1,128,128]{1,2,0:T(8,128)S(1)} custom-call(f32[1,128,128]{2,1,0:T(8,128)S(1)} %fusion.68), custom_call_target="InvertDiagBlocksLowerTriangular" | custom-call | tf_op jit(solution)/shard_map/while/body/eval_jaxpr/triangular_solve | solution.py:14
  113.1 2.2 fusion.69
  115.3 2.5 psum.64
  117.8 0.2 convolution_bitcast_fusion.3
  119.3 0.2 fusion.70
  119.5 2.1 fusion.71
  121.6 0.2 dynamic_update_slice.12
  121.9 0.6 constant_dynamic-slice_fusion.2
  125.1 0.9 fusion.66
  126.2 0.9 fusion.67
  127.1 11.7 %cholesky.78 = f32[128,128]{1,0:T(8,128)S(1)} custom-call(f32[128,128]{1,0:T(8,128)S(1)} %fusion.67), custom_call_target="Cholesky" | custom-call | tf_op jit(solution)/shard_map/while/body/eval_jaxpr/jit(cholesky)/cholesky | solution.py:12
  138.8 0.6 compare_reduce_fusion.2
  139.5 0.7 fusion.68
  140.1 9.8 %custom-call.25 = f32[1,128,128]{1,2,0:T(8,128)S(1)} custom-call(f32[1,128,128]{2,1,0:T(8,128)S(1)} %fusion.68), custom_call_target="InvertDiagBlocksLowerTriangular" | custom-call | tf_op jit(solution)/shard_map/while/body/eval_jaxpr/triangular_solve | solution.py:14
  150.0 2.2 fusion.69
  152.2 2.5 psum.64
  154.7 0.2 convolution_bitcast_fusion.3
  156.2 0.2 fusion.70
  156.4 2.1 fusion.71
  158.5 0.2 dynamic_update_slice.12
  158.8 0.6 constant_dynamic-slice_fusion.2
  162.0 0.9 fusion.66
  163.0 0.9 fusion.67
  164.0 11.7 %cholesky.78 = f32[128,128]{1,0:T(8,128)S(1)} custom-call(f32[128,128]{1,0:T(8,128)S(1)} %fusion.67), custom_call_target="Cholesky" | custom-call | tf_op jit(solution)/shard_map/while/body/eval_jaxpr/jit(cholesky)/cholesky | solution.py:12
  175.7 0.6 compare_reduce_fusion.2
  176.4 0.7 fusion.68
  177.0 9.8 %custom-call.25 = f32[1,128,128]{1,2,0:T(8,128)S(1)} custom-call(f32[1,128,128]{2,1,0:T(8,128)S(1)} %fusion.68), custom_call_target="InvertDiagBlocksLowerTriangular" | custom-call | tf_op jit(solution)/shard_map/while/body/eval_jaxpr/triangular_solve | solution.py:14
  186.9 2.2 fusion.69
  189.1 2.5 psum.64
  191.6 0.2 convolution_bitcast_fusion.3
  193.3 2.1 fusion.71
  195.4 0.2 dynamic_update_slice.12
  195.7 71.7 %psum.57 = f32[8192]{0:T(1024)S(1)} all-reduce(f32[8192]{0:T(1024)S(1)} %get-tuple-element.248), channel_id=1, replica_groups=mesh['dp'=16,'feat'=2] {'dp'}, use_global_device_ids=true, to_apply=%region_7.8 | all-reduce | flops 8192 | bytes 65536 | tf_op jit(solution)/shard_map/psum | solution.py:55
  267.4 0.6 multiply_reduce_fusion
  268.0 3.4 fusion.37
  271.4 2.5 psum.58
  273.9 0.7 fusion.32
  275.3 0.7 fusion.35
  277.9 49.2 %all-reduce.1 = (f32[]{:T(128)}, f32[]{:T(128)}, f32[]{:T(128)}) all-reduce(f32[]{:T(128)S(6)} %mul.160, f32[]{:T(128)S(6)} %mul.165, f32[]{:T(128)S(6)} %mul.168), channel_id=1, replica_groups=mesh['dp'=16,'feat'=2] {'dp','feat'}, use_global_device_ids=true, to_apply=%region_10.11 | all-reduce | flops 3 | bytes 24 | tf_op jit(solution)/shard_map/psum | solution.py:70
  (48 shorter events, 1.3 us)
Async XLA Ops:
  7.2 40.8 %all-reduce.4.cloned.1.call-start = ((), (), s32[]{:S(2)}) async-start(), calls=%async_computation | async-start | bytes 262144 | tf_op jit(solution)/shard_map/psum | solution.py:31
  7.2 6.1 %copy-start.7 = (u32[32]{0:T(128)S(1)}, u32[32]{0:T(128)}, u32[]{:S(2)}) copy-start(u32[32]{0:T(128)} %constant.209) | copy-start | bytes 388
  7.2 40.8 %copy-start = (f32[8192]{0:T(1024)S(1)}, f32[8192]{0:T(1024)}, u32[]{:S(2)}) copy-start(f32[8192]{0:T(1024)} %param.13) | copy-start | bytes 98308
  7.2 40.8 %copy-start.3 = (f32[256]{0:T(256)S(1)}, f32[256]{0:T(256)}, u32[]{:S(2)}) copy-start(f32[256]{0:T(256)} %param.10) | copy-start | bytes 3076
  7.2 40.8 %copy-start.4 = (s32[256]{0:T(256)S(1)}, s32[256]{0:T(256)}, u32[]{:S(2)}) copy-start(s32[256]{0:T(256)} %param.9) | copy-start | bytes 3076
  7.3 40.8 %copy-start.6 = (s32[1,2]{1,0:T(1,128)S(1)}, s32[1,2]{1,0:T(1,128)}, u32[]{:S(2)}) copy-start(s32[1,2]{1,0:T(1,128)} %param.12) | copy-start | bytes 28
  195.7 133.4 %copy-start.2 = (f32[256]{0:T(256)}, f32[256]{0:T(256)S(1)}, u32[]{:S(2)}) copy-start(f32[256]{0:T(256)S(1)} %get-tuple-element.245) | copy-start | bytes 3076
  268.0 61.1 %copy-start.1 = (f32[8192]{0:T(1024)}, f32[8192]{0:T(1024)S(1)}, u32[]{:S(2)}) copy-start(f32[8192]{0:T(1024)S(1)} %get-tuple-element.307) | copy-start | bytes 98308
  273.9 55.2 %copy-start.5 = (f32[256]{0:T(256)}, f32[256]{0:T(256)S(1)}, u32[]{:S(2)}) copy-start(f32[256]{0:T(256)S(1)} %psum.58) | copy-start | bytes 3076
Sparse Core Ops, SparseCore 0:
  12.8 19.3 all-reduce.3
